TPU v7x, 32 devices: a whole 2x2x4 slice. The times are simulated.
32 devices in a mesh: node: 4 (over y, x), row: 8 (over z, core).
Axes of the slice: x: 2, y: 2, z: 4, core: 2. Of those that a mesh axis runs over, the one named last changes fastest.
Arguments:
- inputs: float32 [16, 32, 128, 128], P(None, 'row'), may hold values from -8 to 8
- diagonal: float32 [32, 128, 128], P('row'), may hold values from 0.05 to 1
- observations: float32 [16, 32, 128, 128], P(None, 'row'), may hold values from -0.0078125 to 0.0078125
- frequencies: float32 [4], replicated, may hold values from 0.2 to 3
- weights: float32 [4], replicated, may hold values from 0.5 to 2
- counts: int32 [4], replicated, may hold values from 3 to 6, as said below
- assignment: int32 [4], replicated, may hold values from 0 to 3, each once
Outputs:
- probe_response: float32 [16, 32, 128, 128], P(None, 'row')
- group_gram: float32 [4, 16, 16], P('node')
Inputs may be any that keep to these rules, and one draw needn't show every extreme that they name: `counts`: some node has 6 sweeps and some node 3 in every draw. `assignment`: each node 0 to 3 appears once.
All inputs are finite; a program needn't handle non-finite values.
Results may differ from a plain program's by a relative error of at most 0.0003.
Values sent between devices are 32-bit elements; how exact they have to be, the bound alone decides.
A program may use at most 192 MiB of HBM per device.

v0:
```python
import jax
import jax.numpy as jnp
from jax import lax
from jax.sharding import PartitionSpec as P

NODE_DEV = 1
ITERS = 6


def with_halo(block, sides, width):
    for axis, dim in sides:
        count = lax.axis_size(axis)
        forward = [(i, i + 1) for i in range(count - 1)]
        backward = [(target, source) for source, target in forward]
        low = lax.ppermute(
            lax.slice_in_dim(block, block.shape[dim] - width, None, axis=dim), axis, forward
        )
        high = lax.ppermute(lax.slice_in_dim(block, 0, width, axis=dim), axis, backward)
        block = jnp.concatenate([low, block, high], axis=dim)
    return block


def relax_step(fields, beyond, source, diagonal, shift_col, active):
    padded = jnp.pad(fields, ((0, 0), (0, 0), (0, 0), (0, 0), (1, 1), (1, 1)))
    beside = beyond[:, :, :, 2:] + beyond[:, :, :, :-2]
    beside = beside + padded[:, :, :, :, 2:, 1:-1] + padded[:, :, :, :, :-2, 1:-1]
    beside = beside + padded[:, :, :, :, 1:-1, 2:] + padded[:, :, :, :, 1:-1, :-2]
    diag_full = 6.0 + diagonal
    applied = diag_full * fields - beside
    resid_real = source - applied[:, 0] + shift_col * fields[:, 1]
    resid_imag = -applied[:, 1] - shift_col * fields[:, 0]
    denominator = diag_full * diag_full + shift_col * shift_col
    step_real = (diag_full * resid_real + shift_col * resid_imag) / denominator
    step_imag = (diag_full * resid_imag - shift_col * resid_real) / denominator
    return fields + active * jnp.stack([step_real, step_imag], 1)


def local(inputs, diagonal, observations, frequencies, weights, counts, assignment):
    group_id = lax.axis_index("node")
    my_nodes = lax.dynamic_slice_in_dim(assignment, group_id * NODE_DEV, NODE_DEV)
    quad_count = frequencies.shape[0]
    lookup = my_nodes[:, None] == jnp.arange(quad_count, dtype=jnp.int32)[None, :]
    my_freqs = jnp.sum(jnp.where(lookup, frequencies[None, :], 0.0), 1)
    my_weights = jnp.sum(jnp.where(lookup, weights[None, :], 0.0), 1)
    my_counts = jnp.sum(jnp.where(lookup, counts[None, :], 0), 1)
    planes = inputs.shape[1]
    shift_col = my_freqs.reshape(NODE_DEV, 1, 1, 1, 1)
    start_fields = jnp.zeros((NODE_DEV, 2) + inputs.shape, jnp.float32)

    def sweep_once(sweep, fields):
        beyond = with_halo(fields, (("row", 3),), 1)
        active = (sweep < my_counts).astype(jnp.float32).reshape(NODE_DEV, 1, 1, 1, 1, 1)
        return relax_step(fields, beyond, inputs, diagonal, shift_col, active)

    fields = lax.fori_loop(0, ITERS, sweep_once, start_fields)
    local_cells = planes * inputs.shape[2] * inputs.shape[3]
    flat_fields = fields.reshape(NODE_DEV, 2, inputs.shape[0], local_cells)
    flat_probe = observations.reshape(observations.shape[0], local_cells)
    projected = jnp.einsum(
        "naic,pc->naip", flat_fields, flat_probe, precision=lax.Precision.HIGHEST
    )
    gram_part = jnp.einsum(
        "naic,najc->nij", flat_fields, flat_fields, precision=lax.Precision.HIGHEST
    )
    projected, gram_part = lax.psum((projected, gram_part), "row")
    total_cells = local_cells * lax.axis_size("row")
    group_gram = (
        jnp.einsum("n,nij->ij", my_weights, gram_part, precision=lax.Precision.HIGHEST)
        / total_cells
    )
    weighted = projected * my_weights.reshape(NODE_DEV, 1, 1, 1)
    share = jnp.einsum("naip,naic->pc", weighted, flat_fields, precision=lax.Precision.HIGHEST)
    summed = lax.psum(share, "node")
    probe_response = (summed / quad_count).reshape(observations.shape)
    return (probe_response, group_gram[None])


def solution(mesh):
    placed = (
        P(None, "row", None, None),
        P("row", None, None),
        P(None, "row", None, None),
        P(),
        P(),
        P(),
        P(),
    )
    return jax.shard_map(
        local,
        mesh=mesh,
        in_specs=placed,
        out_specs=(P(None, "row", None, None), P("node", None, None)),
        check_vma=False,
    )
```

profile of v0, /device:TPU:0, one launch (start us, length us, event | category | flops | bytes accessed | tf_op | source)
XLA Modules:
  0.0 677.6 jit_solution(16696439240070895874)
XLA Ops:
  13.5 447.5 %while.16 = (s32[]{:T(128)}, f32[1,2,16,4,128,128]{5,4,3,2,1,0:T(8,128)}, s32[1]{0:T(128)}, f32[4,128,128]{2,1,0:T(8,128)}, f32[16,4,128,128]{3,2,1,0:T(8,128)},...) while((s32[]{:T(128)}, ...), condition=%wide.region_3.4_spmd.clone, body=%wide.region_2.3_spmd.clone.sunk | while | flops 44236800 | bytes 237502864 | solution.py:55
  30.0 24.3 %fusion.25 = f32[1,2,16,4,128,128]{5,4,3,2,1,0:T(8,128)S(1)} fusion(f32[1,2,16,4,128,128]{5,4,3,2,1,0:T(8,128)} %copy-done, f32[1,2,16,1,128,128]{5,4,3,2,1,0:T(8,128)} %collective-permute-done, f32[1,2,16,1,128,128]{5,4,3,2,1,0:T(8,128)} %collective-permute-done.1, f32[4,128,128]{2,1,0:T(8,128)} %get-tuple-element.259), kind=kLoop, calls=%fused_computation.8.clone.1 | loop fusion | flops 18874368 | bytes 21233664 | tf_op jit(solution)/shard_map/while/body/eval_jaxpr/sub | solution.py:29
  54.3 7.1 %add_divide_fusion.2 = (f32[1,1,16,4,128,128]{5,4,3,2,1,0:T(8,128)}, f32[1,1,16,4,128,128]{5,4,3,2,1,0:T(8,128)}) fusion(f32[4,128,128]{2,1,0:T(8,128)} %get-tuple-element.258, f32[]{:T(128)} %bitcast.45, f32[4,128,128]{2,1,0:T(8,128)} %get-tuple-element.259, f32[1,2,16,4,128,128]{5,4,3,2,1,0:T(8,128)S(1)} %bitcast.49, ...), kind=kLoop, calls=%fused_computation.22.clone.1 | loop fusion | flops 14680064 | bytes 29884420 | tf_op jit(solution)/shard_map/while/body/eval_jaxpr/div | solution.py:33
  78.6 25.0 %collective-permute-start = (f32[1,2,16,1,128,128]{5,4,3,2,1,0:T(8,128)}, f32[1,2,16,1,128,128]{5,4,3,2,1,0:T(8,128)}, u32[]{:S(2)}, u32[]{:S(2)}) collective-permute-start(f32[1,2,16,1,128,128]{5,4,3,2,1,0:T(8,128)} %get-tuple-element.260), channel_id=1, source_target_pairs={{0,1},{1,2},{2,3},{3,4},{4,5},{5,6},{6,7},{8,9},{9,10},{10,11},{11... | collective-permute-start | bytes 6291464 | tf_op jit(solution)/shard_map/while/body/eval_jaxpr/ppermute | solution.py:15
  109.8 24.3 %fusion.25 = f32[1,2,16,4,128,128]{5,4,3,2,1,0:T(8,128)S(1)} fusion(f32[1,2,16,4,128,128]{5,4,3,2,1,0:T(8,128)} %copy-done, f32[1,2,16,1,128,128]{5,4,3,2,1,0:T(8,128)} %collective-permute-done, f32[1,2,16,1,128,128]{5,4,3,2,1,0:T(8,128)} %collective-permute-done.1, f32[4,128,128]{2,1,0:T(8,128)} %get-tuple-element.259), kind=kLoop, calls=%fused_computation.8.clone.1 | loop fusion | flops 18874368 | bytes 21233664 | tf_op jit(solution)/shard_map/while/body/eval_jaxpr/sub | solution.py:29
  134.1 7.1 %add_divide_fusion.2 = (f32[1,1,16,4,128,128]{5,4,3,2,1,0:T(8,128)}, f32[1,1,16,4,128,128]{5,4,3,2,1,0:T(8,128)}) fusion(f32[4,128,128]{2,1,0:T(8,128)} %get-tuple-element.258, f32[]{:T(128)} %bitcast.45, f32[4,128,128]{2,1,0:T(8,128)} %get-tuple-element.259, f32[1,2,16,4,128,128]{5,4,3,2,1,0:T(8,128)S(1)} %bitcast.49, ...), kind=kLoop, calls=%fused_computation.22.clone.1 | loop fusion | flops 14680064 | bytes 29884420 | tf_op jit(solution)/shard_map/while/body/eval_jaxpr/div | solution.py:33
  158.3 23.2 %collective-permute-start = (f32[1,2,16,1,128,128]{5,4,3,2,1,0:T(8,128)}, f32[1,2,16,1,128,128]{5,4,3,2,1,0:T(8,128)}, u32[]{:S(2)}, u32[]{:S(2)}) collective-permute-start(f32[1,2,16,1,128,128]{5,4,3,2,1,0:T(8,128)} %get-tuple-element.260), channel_id=1, source_target_pairs={{0,1},{1,2},{2,3},{3,4},{4,5},{5,6},{6,7},{8,9},{9,10},{10,11},{11... | collective-permute-start | bytes 6291464 | tf_op jit(solution)/shard_map/while/body/eval_jaxpr/ppermute | solution.py:15
  187.7 24.3 %fusion.25 = f32[1,2,16,4,128,128]{5,4,3,2,1,0:T(8,128)S(1)} fusion(f32[1,2,16,4,128,128]{5,4,3,2,1,0:T(8,128)} %copy-done, f32[1,2,16,1,128,128]{5,4,3,2,1,0:T(8,128)} %collective-permute-done, f32[1,2,16,1,128,128]{5,4,3,2,1,0:T(8,128)} %collective-permute-done.1, f32[4,128,128]{2,1,0:T(8,128)} %get-tuple-element.259), kind=kLoop, calls=%fused_computation.8.clone.1 | loop fusion | flops 18874368 | bytes 21233664 | tf_op jit(solution)/shard_map/while/body/eval_jaxpr/sub | solution.py:29
  212.0 7.1 %add_divide_fusion.2 = (f32[1,1,16,4,128,128]{5,4,3,2,1,0:T(8,128)}, f32[1,1,16,4,128,128]{5,4,3,2,1,0:T(8,128)}) fusion(f32[4,128,128]{2,1,0:T(8,128)} %get-tuple-element.258, f32[]{:T(128)} %bitcast.45, f32[4,128,128]{2,1,0:T(8,128)} %get-tuple-element.259, f32[1,2,16,4,128,128]{5,4,3,2,1,0:T(8,128)S(1)} %bitcast.49, ...), kind=kLoop, calls=%fused_computation.22.clone.1 | loop fusion | flops 14680064 | bytes 29884420 | tf_op jit(solution)/shard_map/while/body/eval_jaxpr/div | solution.py:33
  236.3 23.2 %collective-permute-start = (f32[1,2,16,1,128,128]{5,4,3,2,1,0:T(8,128)}, f32[1,2,16,1,128,128]{5,4,3,2,1,0:T(8,128)}, u32[]{:S(2)}, u32[]{:S(2)}) collective-permute-start(f32[1,2,16,1,128,128]{5,4,3,2,1,0:T(8,128)} %get-tuple-element.260), channel_id=1, source_target_pairs={{0,1},{1,2},{2,3},{3,4},{4,5},{5,6},{6,7},{8,9},{9,10},{10,11},{11... | collective-permute-start | bytes 6291464 | tf_op jit(solution)/shard_map/while/body/eval_jaxpr/ppermute | solution.py:15
  265.7 24.3 %fusion.25 = f32[1,2,16,4,128,128]{5,4,3,2,1,0:T(8,128)S(1)} fusion(f32[1,2,16,4,128,128]{5,4,3,2,1,0:T(8,128)} %copy-done, f32[1,2,16,1,128,128]{5,4,3,2,1,0:T(8,128)} %collective-permute-done, f32[1,2,16,1,128,128]{5,4,3,2,1,0:T(8,128)} %collective-permute-done.1, f32[4,128,128]{2,1,0:T(8,128)} %get-tuple-element.259), kind=kLoop, calls=%fused_computation.8.clone.1 | loop fusion | flops 18874368 | bytes 21233664 | tf_op jit(solution)/shard_map/while/body/eval_jaxpr/sub | solution.py:29
  290.0 7.1 %add_divide_fusion.2 = (f32[1,1,16,4,128,128]{5,4,3,2,1,0:T(8,128)}, f32[1,1,16,4,128,128]{5,4,3,2,1,0:T(8,128)}) fusion(f32[4,128,128]{2,1,0:T(8,128)} %get-tuple-element.258, f32[]{:T(128)} %bitcast.45, f32[4,128,128]{2,1,0:T(8,128)} %get-tuple-element.259, f32[1,2,16,4,128,128]{5,4,3,2,1,0:T(8,128)S(1)} %bitcast.49, ...), kind=kLoop, calls=%fused_computation.22.clone.1 | loop fusion | flops 14680064 | bytes 29884420 | tf_op jit(solution)/shard_map/while/body/eval_jaxpr/div | solution.py:33
  314.2 23.2 %collective-permute-start = (f32[1,2,16,1,128,128]{5,4,3,2,1,0:T(8,128)}, f32[1,2,16,1,128,128]{5,4,3,2,1,0:T(8,128)}, u32[]{:S(2)}, u32[]{:S(2)}) collective-permute-start(f32[1,2,16,1,128,128]{5,4,3,2,1,0:T(8,128)} %get-tuple-element.260), channel_id=1, source_target_pairs={{0,1},{1,2},{2,3},{3,4},{4,5},{5,6},{6,7},{8,9},{9,10},{10,11},{11... | collective-permute-start | bytes 6291464 | tf_op jit(solution)/shard_map/while/body/eval_jaxpr/ppermute | solution.py:15
  343.6 24.3 %fusion.25 = f32[1,2,16,4,128,128]{5,4,3,2,1,0:T(8,128)S(1)} fusion(f32[1,2,16,4,128,128]{5,4,3,2,1,0:T(8,128)} %copy-done, f32[1,2,16,1,128,128]{5,4,3,2,1,0:T(8,128)} %collective-permute-done, f32[1,2,16,1,128,128]{5,4,3,2,1,0:T(8,128)} %collective-permute-done.1, f32[4,128,128]{2,1,0:T(8,128)} %get-tuple-element.259), kind=kLoop, calls=%fused_computation.8.clone.1 | loop fusion | flops 18874368 | bytes 21233664 | tf_op jit(solution)/shard_map/while/body/eval_jaxpr/sub | solution.py:29
  367.9 7.1 %add_divide_fusion.2 = (f32[1,1,16,4,128,128]{5,4,3,2,1,0:T(8,128)}, f32[1,1,16,4,128,128]{5,4,3,2,1,0:T(8,128)}) fusion(f32[4,128,128]{2,1,0:T(8,128)} %get-tuple-element.258, f32[]{:T(128)} %bitcast.45, f32[4,128,128]{2,1,0:T(8,128)} %get-tuple-element.259, f32[1,2,16,4,128,128]{5,4,3,2,1,0:T(8,128)S(1)} %bitcast.49, ...), kind=kLoop, calls=%fused_computation.22.clone.1 | loop fusion | flops 14680064 | bytes 29884420 | tf_op jit(solution)/shard_map/while/body/eval_jaxpr/div | solution.py:33
  392.2 23.2 %collective-permute-start = (f32[1,2,16,1,128,128]{5,4,3,2,1,0:T(8,128)}, f32[1,2,16,1,128,128]{5,4,3,2,1,0:T(8,128)}, u32[]{:S(2)}, u32[]{:S(2)}) collective-permute-start(f32[1,2,16,1,128,128]{5,4,3,2,1,0:T(8,128)} %get-tuple-element.260), channel_id=1, source_target_pairs={{0,1},{1,2},{2,3},{3,4},{4,5},{5,6},{6,7},{8,9},{9,10},{10,11},{11... | collective-permute-start | bytes 6291464 | tf_op jit(solution)/shard_map/while/body/eval_jaxpr/ppermute | solution.py:15
  421.6 24.3 %fusion.25 = f32[1,2,16,4,128,128]{5,4,3,2,1,0:T(8,128)S(1)} fusion(f32[1,2,16,4,128,128]{5,4,3,2,1,0:T(8,128)} %copy-done, f32[1,2,16,1,128,128]{5,4,3,2,1,0:T(8,128)} %collective-permute-done, f32[1,2,16,1,128,128]{5,4,3,2,1,0:T(8,128)} %collective-permute-done.1, f32[4,128,128]{2,1,0:T(8,128)} %get-tuple-element.259), kind=kLoop, calls=%fused_computation.8.clone.1 | loop fusion | flops 18874368 | bytes 21233664 | tf_op jit(solution)/shard_map/while/body/eval_jaxpr/sub | solution.py:29
  445.9 7.1 %add_divide_fusion.2 = (f32[1,1,16,4,128,128]{5,4,3,2,1,0:T(8,128)}, f32[1,1,16,4,128,128]{5,4,3,2,1,0:T(8,128)}) fusion(f32[4,128,128]{2,1,0:T(8,128)} %get-tuple-element.258, f32[]{:T(128)} %bitcast.45, f32[4,128,128]{2,1,0:T(8,128)} %get-tuple-element.259, f32[1,2,16,4,128,128]{5,4,3,2,1,0:T(8,128)S(1)} %bitcast.49, ...), kind=kLoop, calls=%fused_computation.22.clone.1 | loop fusion | flops 14680064 | bytes 29884420 | tf_op jit(solution)/shard_map/while/body/eval_jaxpr/div | solution.py:33
  461.0 7.5 %reshape.188 = f32[2,16,65536]{2,1,0:T(8,128)} reshape(f32[1,2,16,4,128,128]{5,4,3,2,1,0:T(8,128)} %get-tuple-element.162) | data formatting | bytes 16777216 | tf_op jit(solution)/shard_map/reshape.4
  472.4 27.3 %fusion.11 = f32[1,16,16]{2,1,0:T(8,128)S(1)} fusion(f32[2,16,4,128,128]{4,3,2,1,0:T(8,128)} %bitcast.52), kind=kOutput, calls=%fused_computation.30 | convolution fusion | flops 402653184 | bytes 8389632 | tf_op jit(solution)/shard_map/naic,najc->nij/dot_general | solution.py:62
  501.0 8.4 %convolution_bitcast_fusion.1 = f32[1,2,16,16]{3,2,1,0:T(8,128)S(1)} fusion(f32[2,16,65536]{2,1,0:T(8,128)S(1)} %copy-done.2, f32[16,65536,1]{1,0,2:T(8,128)} %reshape.196), kind=kOutput, calls=%fused_computation.29 | convolution fusion | flops 402653184 | bytes 12584960 | tf_op jit(solution)/shard_map/naic,pc->naip/dot_general | solution.py:59
  509.4 45.7 %all-reduce.1 = (f32[1,2,16,16]{3,2,1,0:T(8,128)S(1)}, f32[1,16,16]{2,1,0:T(8,128)S(1)}) all-reduce(f32[1,2,16,16]{3,2,1,0:T(8,128)S(1)} %convolution_bitcast_fusion.1, f32[1,16,16]{2,1,0:T(8,128)S(1)} %fusion.11), channel_id=1, replica_groups=mesh['node'=4,'row'=8] {'row'}, use_global_device_ids=true, to_apply=%region_4.5 | all-reduce | flops 768 | bytes 6144 | tf_op jit(solution)/shard_map/psum | solution.py:65
  555.2 8.4 %convolution_bitcast_fusion = f32[16,65536]{1,0:T(8,128)} fusion(f32[2,16,65536]{2,1,0:T(8,128)} %reshape.188, f32[1,2,16,16]{3,2,1,0:T(8,128)S(1)} %get-tuple-element.201, f32[]{:T(128)} %select_reduce_fusion), kind=kOutput, calls=%fused_computation.25 | convolution fusion | flops 402653696 | bytes 12584964 | tf_op jit(solution)/shard_map/naip,naic->pc/dot_general | solution.py:72
  564.8 100.7 %all-reduce.4.cloned.1.call-done = f32[16,65536]{1,0:T(8,128)} async-done(((f32[16,65536]{1,0:T(8,128)}), f32[16,65536]{1,0:T(8,128)}) %all-reduce.4.cloned.1.call-update) | async-done | bytes 4194320 | tf_op jit(solution)/shard_map/psum | solution.py:73
  (154 shorter events, 153.5 us)
Async XLA Ops:
  7.2 658.4 %all-reduce.4.cloned.1.call-start = ((), (), s32[]{:S(2)}) async-start(), calls=%async_computation | async-start | bytes 8388608 | tf_op jit(solution)/shard_map/psum | solution.py:73
  19.3 6.6 collective-permute-start
  23.0 7.0 %collective-permute-start.1 = (f32[1,2,16,1,128,128]{5,4,3,2,1,0:T(8,128)S(1)}, f32[1,2,16,1,128,128]{5,4,3,2,1,0:T(8,128)}, u32[]{:S(2)}, u32[]{:S(2)}) collective-permute-start(f32[1,2,16,1,128,128]{5,4,3,2,1,0:T(8,128)S(1)} %get-tuple-element.261), channel_id=1, source_target_pairs={{1,0},{2,1},{3,2},{4,3},{5,4},{6,5},{7,6},{9,8},{10,9},{11,10},{12... | collective-permute-start | bytes 6291464 | tf_op jit(solution)/shard_map/while/body/eval_jaxpr/ppermute | solution.py:18
  25.0 29.3 %slice-start = ((s8[8388608]{0:T(1024)(128)(4,1)}), s8[4194304]{0:T(1024)(128)(4,1)S(1)}, s32[]{:S(2)}) async-start(s8[8388608]{0:T(1024)(128)(4,1)} %bitcast.48), calls=%async_computation.1 | async-start | bytes 8388608 | tf_op jit(solution)/shard_map/while
  30.0 31.5 %slice-start.2 = ((s8[8388608]{0:T(1024)(128)(4,1)}), s8[4194304]{0:T(1024)(128)(4,1)S(1)}, s32[]{:S(2)}) async-start(s8[8388608]{0:T(1024)(128)(4,1)} %bitcast.50), calls=%async_computation.3 | async-start | bytes 8388608 | tf_op jit(solution)/shard_map/while
  76.9 28.7 %copy-start.3 = (f32[4,128,128]{2,1,0:T(8,128)S(1)}, f32[4,128,128]{2,1,0:T(8,128)}, u32[]{:S(2)}) copy-start(f32[4,128,128]{2,1,0:T(8,128)} %get-tuple-element.285) | copy-start | bytes 786436 | tf_op jit(solution)/shard_map/while
  78.6 27.9 %collective-permute-start = (f32[1,2,16,1,128,128]{5,4,3,2,1,0:T(8,128)}, f32[1,2,16,1,128,128]{5,4,3,2,1,0:T(8,128)}, u32[]{:S(2)}, u32[]{:S(2)}) collective-permute-start(f32[1,2,16,1,128,128]{5,4,3,2,1,0:T(8,128)} %get-tuple-element.260), channel_id=1, source_target_pairs={{0,1},{1,2},{2,3},{3,4},{4,5},{5,6},{6,7},{8,9},{9,10},{10,11},{11... | collective-permute-start | bytes 6291464 | tf_op jit(solution)/shard_map/while/body/eval_jaxpr/ppermute | solution.py:15
  103.6 6.2 collective-permute-start.1
  105.6 28.5 %slice-start = ((s8[8388608]{0:T(1024)(128)(4,1)}), s8[4194304]{0:T(1024)(128)(4,1)S(1)}, s32[]{:S(2)}) async-start(s8[8388608]{0:T(1024)(128)(4,1)} %bitcast.48), calls=%async_computation.1 | async-start | bytes 8388608 | tf_op jit(solution)/shard_map/while
  109.8 31.5 %slice-start.2 = ((s8[8388608]{0:T(1024)(128)(4,1)}), s8[4194304]{0:T(1024)(128)(4,1)S(1)}, s32[]{:S(2)}) async-start(s8[8388608]{0:T(1024)(128)(4,1)} %bitcast.50), calls=%async_computation.3 | async-start | bytes 8388608 | tf_op jit(solution)/shard_map/while
  158.3 26.0 %collective-permute-start = (f32[1,2,16,1,128,128]{5,4,3,2,1,0:T(8,128)}, f32[1,2,16,1,128,128]{5,4,3,2,1,0:T(8,128)}, u32[]{:S(2)}, u32[]{:S(2)}) collective-permute-start(f32[1,2,16,1,128,128]{5,4,3,2,1,0:T(8,128)} %get-tuple-element.260), channel_id=1, source_target_pairs={{0,1},{1,2},{2,3},{3,4},{4,5},{5,6},{6,7},{8,9},{9,10},{10,11},{11... | collective-permute-start | bytes 6291464 | tf_op jit(solution)/shard_map/while/body/eval_jaxpr/ppermute | solution.py:15
  181.5 6.2 collective-permute-start.1
  187.7 31.5 %slice-start.2 = ((s8[8388608]{0:T(1024)(128)(4,1)}), s8[4194304]{0:T(1024)(128)(4,1)S(1)}, s32[]{:S(2)}) async-start(s8[8388608]{0:T(1024)(128)(4,1)} %bitcast.50), calls=%async_computation.3 | async-start | bytes 8388608 | tf_op jit(solution)/shard_map/while
  236.3 26.0 %collective-permute-start = (f32[1,2,16,1,128,128]{5,4,3,2,1,0:T(8,128)}, f32[1,2,16,1,128,128]{5,4,3,2,1,0:T(8,128)}, u32[]{:S(2)}, u32[]{:S(2)}) collective-permute-start(f32[1,2,16,1,128,128]{5,4,3,2,1,0:T(8,128)} %get-tuple-element.260), channel_id=1, source_target_pairs={{0,1},{1,2},{2,3},{3,4},{4,5},{5,6},{6,7},{8,9},{9,10},{10,11},{11... | collective-permute-start | bytes 6291464 | tf_op jit(solution)/shard_map/while/body/eval_jaxpr/ppermute | solution.py:15
  259.5 6.2 collective-permute-start.1
  265.7 31.5 %slice-start.2 = ((s8[8388608]{0:T(1024)(128)(4,1)}), s8[4194304]{0:T(1024)(128)(4,1)S(1)}, s32[]{:S(2)}) async-start(s8[8388608]{0:T(1024)(128)(4,1)} %bitcast.50), calls=%async_computation.3 | async-start | bytes 8388608 | tf_op jit(solution)/shard_map/while
  314.2 26.0 %collective-permute-start = (f32[1,2,16,1,128,128]{5,4,3,2,1,0:T(8,128)}, f32[1,2,16,1,128,128]{5,4,3,2,1,0:T(8,128)}, u32[]{:S(2)}, u32[]{:S(2)}) collective-permute-start(f32[1,2,16,1,128,128]{5,4,3,2,1,0:T(8,128)} %get-tuple-element.260), channel_id=1, source_target_pairs={{0,1},{1,2},{2,3},{3,4},{4,5},{5,6},{6,7},{8,9},{9,10},{10,11},{11... | collective-permute-start | bytes 6291464 | tf_op jit(solution)/shard_map/while/body/eval_jaxpr/ppermute | solution.py:15
  337.4 6.2 collective-permute-start.1
  343.6 31.5 %slice-start.2 = ((s8[8388608]{0:T(1024)(128)(4,1)}), s8[4194304]{0:T(1024)(128)(4,1)S(1)}, s32[]{:S(2)}) async-start(s8[8388608]{0:T(1024)(128)(4,1)} %bitcast.50), calls=%async_computation.3 | async-start | bytes 8388608 | tf_op jit(solution)/shard_map/while
  392.2 26.0 %collective-permute-start = (f32[1,2,16,1,128,128]{5,4,3,2,1,0:T(8,128)}, f32[1,2,16,1,128,128]{5,4,3,2,1,0:T(8,128)}, u32[]{:S(2)}, u32[]{:S(2)}) collective-permute-start(f32[1,2,16,1,128,128]{5,4,3,2,1,0:T(8,128)} %get-tuple-element.260), channel_id=1, source_target_pairs={{0,1},{1,2},{2,3},{3,4},{4,5},{5,6},{6,7},{8,9},{9,10},{10,11},{11... | collective-permute-start | bytes 6291464 | tf_op jit(solution)/shard_map/while/body/eval_jaxpr/ppermute | solution.py:15
  415.4 6.2 collective-permute-start.1
  421.6 31.5 %slice-start.2 = ((s8[8388608]{0:T(1024)(128)(4,1)}), s8[4194304]{0:T(1024)(128)(4,1)S(1)}, s32[]{:S(2)}) async-start(s8[8388608]{0:T(1024)(128)(4,1)} %bitcast.50), calls=%async_computation.3 | async-start | bytes 8388608 | tf_op jit(solution)/shard_map/while
  468.5 31.3 %copy-start.4 = (f32[4]{0:T(128)S(1)}, f32[4]{0:T(128)}, u32[]{:S(2)}) copy-start(f32[4]{0:T(128)} %param.13) | copy-start | bytes 52
  472.4 28.5 %copy-start.2 = (f32[2,16,65536]{2,1,0:T(8,128)S(1)}, f32[2,16,65536]{2,1,0:T(8,128)}, u32[]{:S(2)}) copy-start(f32[2,16,65536]{2,1,0:T(8,128)} %reshape.188) | copy-start | bytes 25165828
  (33 other events, 456.3 us)
Sparse Core Ops, SparseCore 0:
  563.7 101.8 all-reduce.3
where the time goes:
time: 678 us
  other arithmetic  252 us (37%)
  starting transfers between devices  129 us (19%)
  waiting for transfers between devices  122 us (18%)
  local copies, waits for them, and re-layouts  64.7 us (10%)
  blocking collectives  45.7 us (7%)
  matrix products  44.1 us (7%)
  between operations  15.2 us (2%)
    sub x6, other arithmetic, relax_step(): applied = diag_full * fields - beside  146 us
    ppermute x6, starting transfers between devices, with_halo(): lax.ppermute(lax.slice_in_dim(block, block.shape[dim] - width, None, axis...  122 us
    psum x1, waiting for transfers between devices, local(): summed = lax.psum(share, 'node')  101 us
    psum x1, blocking collectives, local(): projected, gram_part = lax.psum((projected, gram_part), 'row')  45.7 us
    div x6, other arithmetic, relax_step(): step_real = (diag_full * resid_real + shift_col * resid_imag) / denominator  42.9 us
    while x84, local copies, waits for them, and re-layouts  38.8 us
    add x6, other arithmetic, relax_step(): return fields + active * jnp.stack([step_real, step_imag], 1)  28 us
    dot_general x1, matrix products, local(): jnp.einsum('naic,najc->nij', flat_fields, flat_fields, precision=lax.Prec...  27.3 us
  transfers between devices with their start and end apart: 13, of which 7 were waited for; matrix products, arithmetic and copies ran while one was open for 1% of the time, Pallas kernels for 0%

commit v1 on v0

--- a/solution.py
+++ b/solution.py
@@ -70,7 +70,7 @@
     )
     weighted = projected * my_weights.reshape(NODE_DEV, 1, 1, 1)
     share = jnp.einsum("naip,naic->pc", weighted, flat_fields, precision=lax.Precision.HIGHEST)
-    summed = lax.psum(share, "node")
+    summed = jnp.sum(lax.all_gather(share, "node"), axis=0)
     probe_response = (summed / quad_count).reshape(observations.shape)
     return (probe_response, group_gram[None])
 

time: 678 us -> 741 us (1.093)
  waiting for transfers between devices: 122 us -> 175 us
  other arithmetic: 252 us -> 261 us
    all_gather x0 -> x1, waiting for transfers between devices: none -> 155 us  [local(): summed = jnp.sum(lax.all_gather(share, 'node'), axis=0)]
    psum x1 -> x0, waiting for transfers between devices: 101 us -> none  [local(): summed = lax.psum(share, 'node')]
    reduce_sum x0 -> x1, other arithmetic: none -> 9.15 us  [local(): summed = jnp.sum(lax.all_gather(share, 'node'), axis=0)]
where the time goes in v1:
time: 741 us; the launch traced here: 740 us
  other arithmetic  261 us (35%)
  waiting for transfers between devices  175 us (24%)
  starting transfers between devices  129 us (17%)
  local copies, waits for them, and re-layouts  64.7 us (9%)
  blocking collectives  45.7 us (6%)
  matrix products  44 us (6%)
  between operations  15.2 us (2%)
    all_gather x1, waiting for transfers between devices, local(): summed = jnp.sum(lax.all_gather(share, 'node'), axis=0)  155 us
    sub x6, other arithmetic, relax_step(): applied = diag_full * fields - beside  146 us
    ppermute x6, starting transfers between devices, with_halo(): lax.ppermute(lax.slice_in_dim(block, block.shape[dim] - width, None, axis...  122 us
    psum x1, blocking collectives, local(): projected, gram_part = lax.psum((projected, gram_part), 'row')  45.7 us
    div x6, other arithmetic, relax_step(): step_real = (diag_full * resid_real + shift_col * resid_imag) / denominator  42.9 us
    while x84, local copies, waits for them, and re-layouts  38.8 us
    add x6, other arithmetic, relax_step(): return fields + active * jnp.stack([step_real, step_imag], 1)  28 us
    dot_general x1, matrix products, local(): jnp.einsum('naic,najc->nij', flat_fields, flat_fields, precision=lax.Prec...  27.3 us
  transfers between devices with their start and end apart: 13, of which 7 were waited for; matrix products, arithmetic and copies ran while one was open for 1% of the time, Pallas kernels for 0%

profile of v1, /device:TPU:0, one launch (start us, length us, event | category | flops | bytes accessed | tf_op | source)
XLA Modules:
  0.0 740.3 jit_solution(13182935443926719086)
XLA Ops:
  13.5 447.5 %while.16 = (s32[]{:T(128)}, f32[1,2,16,4,128,128]{5,4,3,2,1,0:T(8,128)}, s32[1]{0:T(128)}, f32[4,128,128]{2,1,0:T(8,128)}, f32[16,4,128,128]{3,2,1,0:T(8,128)},...) while((s32[]{:T(128)}, ...), condition=%wide.region_3.4_spmd.clone, body=%wide.region_2.3_spmd.clone.sunk | while | flops 44236800 | bytes 237502864 | solution.py:55
  30.0 24.3 %fusion.25 = f32[1,2,16,4,128,128]{5,4,3,2,1,0:T(8,128)S(1)} fusion(f32[1,2,16,4,128,128]{5,4,3,2,1,0:T(8,128)} %copy-done, f32[1,2,16,1,128,128]{5,4,3,2,1,0:T(8,128)} %collective-permute-done, f32[1,2,16,1,128,128]{5,4,3,2,1,0:T(8,128)} %collective-permute-done.1, f32[4,128,128]{2,1,0:T(8,128)} %get-tuple-element.259), kind=kLoop, calls=%fused_computation.8.clone.1 | loop fusion | flops 18874368 | bytes 21233664 | tf_op jit(solution)/shard_map/while/body/eval_jaxpr/sub | solution.py:29
  54.3 7.1 add_divide_fusion.2
  78.6 25.0 %collective-permute-start = (f32[1,2,16,1,128,128]{5,4,3,2,1,0:T(8,128)}, f32[1,2,16,1,128,128]{5,4,3,2,1,0:T(8,128)}, u32[]{:S(2)}, u32[]{:S(2)}) collective-permute-start(f32[1,2,16,1,128,128]{5,4,3,2,1,0:T(8,128)} %get-tuple-element.260), channel_id=1, source_target_pairs={{0,1},{1,2},{2,3},{3,4},{4,5},{5,6},{6,7},{8,9},{9,10},{10,11},{11... | collective-permute-start | bytes 6291464 | tf_op jit(solution)/shard_map/while/body/eval_jaxpr/ppermute | solution.py:15
  109.8 24.3 %fusion.25 = f32[1,2,16,4,128,128]{5,4,3,2,1,0:T(8,128)S(1)} fusion(f32[1,2,16,4,128,128]{5,4,3,2,1,0:T(8,128)} %copy-done, f32[1,2,16,1,128,128]{5,4,3,2,1,0:T(8,128)} %collective-permute-done, f32[1,2,16,1,128,128]{5,4,3,2,1,0:T(8,128)} %collective-permute-done.1, f32[4,128,128]{2,1,0:T(8,128)} %get-tuple-element.259), kind=kLoop, calls=%fused_computation.8.clone.1 | loop fusion | flops 18874368 | bytes 21233664 | tf_op jit(solution)/shard_map/while/body/eval_jaxpr/sub | solution.py:29
  134.1 7.1 add_divide_fusion.2
  158.3 23.2 %collective-permute-start = (f32[1,2,16,1,128,128]{5,4,3,2,1,0:T(8,128)}, f32[1,2,16,1,128,128]{5,4,3,2,1,0:T(8,128)}, u32[]{:S(2)}, u32[]{:S(2)}) collective-permute-start(f32[1,2,16,1,128,128]{5,4,3,2,1,0:T(8,128)} %get-tuple-element.260), channel_id=1, source_target_pairs={{0,1},{1,2},{2,3},{3,4},{4,5},{5,6},{6,7},{8,9},{9,10},{10,11},{11... | collective-permute-start | bytes 6291464 | tf_op jit(solution)/shard_map/while/body/eval_jaxpr/ppermute | solution.py:15
  187.7 24.3 %fusion.25 = f32[1,2,16,4,128,128]{5,4,3,2,1,0:T(8,128)S(1)} fusion(f32[1,2,16,4,128,128]{5,4,3,2,1,0:T(8,128)} %copy-done, f32[1,2,16,1,128,128]{5,4,3,2,1,0:T(8,128)} %collective-permute-done, f32[1,2,16,1,128,128]{5,4,3,2,1,0:T(8,128)} %collective-permute-done.1, f32[4,128,128]{2,1,0:T(8,128)} %get-tuple-element.259), kind=kLoop, calls=%fused_computation.8.clone.1 | loop fusion | flops 18874368 | bytes 21233664 | tf_op jit(solution)/shard_map/while/body/eval_jaxpr/sub | solution.py:29
  212.0 7.1 add_divide_fusion.2
  236.3 23.2 %collective-permute-start = (f32[1,2,16,1,128,128]{5,4,3,2,1,0:T(8,128)}, f32[1,2,16,1,128,128]{5,4,3,2,1,0:T(8,128)}, u32[]{:S(2)}, u32[]{:S(2)}) collective-permute-start(f32[1,2,16,1,128,128]{5,4,3,2,1,0:T(8,128)} %get-tuple-element.260), channel_id=1, source_target_pairs={{0,1},{1,2},{2,3},{3,4},{4,5},{5,6},{6,7},{8,9},{9,10},{10,11},{11... | collective-permute-start | bytes 6291464 | tf_op jit(solution)/shard_map/while/body/eval_jaxpr/ppermute | solution.py:15
  265.7 24.3 %fusion.25 = f32[1,2,16,4,128,128]{5,4,3,2,1,0:T(8,128)S(1)} fusion(f32[1,2,16,4,128,128]{5,4,3,2,1,0:T(8,128)} %copy-done, f32[1,2,16,1,128,128]{5,4,3,2,1,0:T(8,128)} %collective-permute-done, f32[1,2,16,1,128,128]{5,4,3,2,1,0:T(8,128)} %collective-permute-done.1, f32[4,128,128]{2,1,0:T(8,128)} %get-tuple-element.259), kind=kLoop, calls=%fused_computation.8.clone.1 | loop fusion | flops 18874368 | bytes 21233664 | tf_op jit(solution)/shard_map/while/body/eval_jaxpr/sub | solution.py:29
  290.0 7.1 add_divide_fusion.2
  314.2 23.2 %collective-permute-start = (f32[1,2,16,1,128,128]{5,4,3,2,1,0:T(8,128)}, f32[1,2,16,1,128,128]{5,4,3,2,1,0:T(8,128)}, u32[]{:S(2)}, u32[]{:S(2)}) collective-permute-start(f32[1,2,16,1,128,128]{5,4,3,2,1,0:T(8,128)} %get-tuple-element.260), channel_id=1, source_target_pairs={{0,1},{1,2},{2,3},{3,4},{4,5},{5,6},{6,7},{8,9},{9,10},{10,11},{11... | collective-permute-start | bytes 6291464 | tf_op jit(solution)/shard_map/while/body/eval_jaxpr/ppermute | solution.py:15
  343.6 24.3 %fusion.25 = f32[1,2,16,4,128,128]{5,4,3,2,1,0:T(8,128)S(1)} fusion(f32[1,2,16,4,128,128]{5,4,3,2,1,0:T(8,128)} %copy-done, f32[1,2,16,1,128,128]{5,4,3,2,1,0:T(8,128)} %collective-permute-done, f32[1,2,16,1,128,128]{5,4,3,2,1,0:T(8,128)} %collective-permute-done.1, f32[4,128,128]{2,1,0:T(8,128)} %get-tuple-element.259), kind=kLoop, calls=%fused_computation.8.clone.1 | loop fusion | flops 18874368 | bytes 21233664 | tf_op jit(solution)/shard_map/while/body/eval_jaxpr/sub | solution.py:29
  367.9 7.1 add_divide_fusion.2
  392.2 23.2 %collective-permute-start = (f32[1,2,16,1,128,128]{5,4,3,2,1,0:T(8,128)}, f32[1,2,16,1,128,128]{5,4,3,2,1,0:T(8,128)}, u32[]{:S(2)}, u32[]{:S(2)}) collective-permute-start(f32[1,2,16,1,128,128]{5,4,3,2,1,0:T(8,128)} %get-tuple-element.260), channel_id=1, source_target_pairs={{0,1},{1,2},{2,3},{3,4},{4,5},{5,6},{6,7},{8,9},{9,10},{10,11},{11... | collective-permute-start | bytes 6291464 | tf_op jit(solution)/shard_map/while/body/eval_jaxpr/ppermute | solution.py:15
  421.6 24.3 %fusion.25 = f32[1,2,16,4,128,128]{5,4,3,2,1,0:T(8,128)S(1)} fusion(f32[1,2,16,4,128,128]{5,4,3,2,1,0:T(8,128)} %copy-done, f32[1,2,16,1,128,128]{5,4,3,2,1,0:T(8,128)} %collective-permute-done, f32[1,2,16,1,128,128]{5,4,3,2,1,0:T(8,128)} %collective-permute-done.1, f32[4,128,128]{2,1,0:T(8,128)} %get-tuple-element.259), kind=kLoop, calls=%fused_computation.8.clone.1 | loop fusion | flops 18874368 | bytes 21233664 | tf_op jit(solution)/shard_map/while/body/eval_jaxpr/sub | solution.py:29
  461.0 7.5 %reshape.189 = f32[2,16,65536]{2,1,0:T(8,128)} reshape(f32[1,2,16,4,128,128]{5,4,3,2,1,0:T(8,128)} %get-tuple-element.162) | data formatting | bytes 16777216 | tf_op jit(solution)/shard_map/reshape.4
  472.4 27.3 %fusion.11 = f32[1,16,16]{2,1,0:T(8,128)S(1)} fusion(f32[2,16,4,128,128]{4,3,2,1,0:T(8,128)} %bitcast.53), kind=kOutput, calls=%fused_computation.30 | convolution fusion | flops 402653184 | bytes 8389632 | tf_op jit(solution)/shard_map/naic,najc->nij/dot_general | solution.py:62
  500.9 8.4 %convolution_bitcast_fusion.1 = f32[1,2,16,16]{3,2,1,0:T(8,128)S(1)} fusion(f32[2,16,65536]{2,1,0:T(8,128)S(1)} %copy-done.2, f32[16,65536,1]{1,0,2:T(8,128)} %reshape.197), kind=kOutput, calls=%fused_computation.29 | convolution fusion | flops 402653184 | bytes 12584960 | tf_op jit(solution)/shard_map/naic,pc->naip/dot_general | solution.py:59
  509.4 45.7 %all-reduce.1 = (f32[1,2,16,16]{3,2,1,0:T(8,128)S(1)}, f32[1,16,16]{2,1,0:T(8,128)S(1)}) all-reduce(f32[1,2,16,16]{3,2,1,0:T(8,128)S(1)} %convolution_bitcast_fusion.1, f32[1,16,16]{2,1,0:T(8,128)S(1)} %fusion.11), channel_id=1, replica_groups=mesh['node'=4,'row'=8] {'row'}, use_global_device_ids=true, to_apply=%region_4.5 | all-reduce | flops 768 | bytes 6144 | tf_op jit(solution)/shard_map/psum | solution.py:65
  555.1 8.3 %convolution_bitcast_fusion = f32[16,65536]{1,0:T(8,128)} fusion(f32[2,16,65536]{2,1,0:T(8,128)} %reshape.189, f32[1,2,16,16]{3,2,1,0:T(8,128)S(1)} %get-tuple-element.201, f32[]{:T(128)} %select_reduce_fusion), kind=kOutput, calls=%fused_computation.25 | convolution fusion | flops 402653696 | bytes 12584964 | tf_op jit(solution)/shard_map/naip,naic->pc/dot_general | solution.py:72
  564.5 154.5 %all-gather.3.cloned.1.call-done = f32[64,65536]{1,0:T(8,128)} async-done(((f32[16,65536]{1,0:T(8,128)}), f32[64,65536]{1,0:T(8,128)}) %all-gather.3.cloned.1.call-update) | async-done | bytes 16777232 | tf_op jit(solution)/shard_map/all_gather | solution.py:73
  719.1 9.1 %reduce_sum.42 = f32[16,65536]{1,0:T(8,128)} reduce(f32[4,16,65536]{2,1,0:T(8,128)} %bitcast.54, f32[]{:T(128)} %constant.47.clone.1), dimensions={0}, to_apply=%region_6.7 | reduce | flops 3145728 | bytes 20971524 | tf_op jit(solution)/shard_map/reduce_sum | solution.py:73
  (155 shorter events, 160.5 us)
Async XLA Ops:
  7.2 711.9 %all-gather.3.cloned.1.call-start = ((), (), s32[]{:S(2)}) async-start(), calls=%async_computation | async-start | bytes 20971520 | tf_op jit(solution)/shard_map/all_gather | solution.py:73
  19.3 6.6 collective-permute-start
  23.0 7.0 collective-permute-start.1
  25.0 29.3 %slice-start = ((s8[8388608]{0:T(1024)(128)(4,1)}), s8[4194304]{0:T(1024)(128)(4,1)S(1)}, s32[]{:S(2)}) async-start(s8[8388608]{0:T(1024)(128)(4,1)} %bitcast.49), calls=%async_computation.1 | async-start | bytes 8388608 | tf_op jit(solution)/shard_map/while
  30.0 31.5 %slice-start.2 = ((s8[8388608]{0:T(1024)(128)(4,1)}), s8[4194304]{0:T(1024)(128)(4,1)S(1)}, s32[]{:S(2)}) async-start(s8[8388608]{0:T(1024)(128)(4,1)} %bitcast.51), calls=%async_computation.3 | async-start | bytes 8388608 | tf_op jit(solution)/shard_map/while
  76.9 28.7 %copy-start.3 = (f32[4,128,128]{2,1,0:T(8,128)S(1)}, f32[4,128,128]{2,1,0:T(8,128)}, u32[]{:S(2)}) copy-start(f32[4,128,128]{2,1,0:T(8,128)} %get-tuple-element.285) | copy-start | bytes 786436 | tf_op jit(solution)/shard_map/while
  78.6 27.9 %collective-permute-start = (f32[1,2,16,1,128,128]{5,4,3,2,1,0:T(8,128)}, f32[1,2,16,1,128,128]{5,4,3,2,1,0:T(8,128)}, u32[]{:S(2)}, u32[]{:S(2)}) collective-permute-start(f32[1,2,16,1,128,128]{5,4,3,2,1,0:T(8,128)} %get-tuple-element.260), channel_id=1, source_target_pairs={{0,1},{1,2},{2,3},{3,4},{4,5},{5,6},{6,7},{8,9},{9,10},{10,11},{11... | collective-permute-start | bytes 6291464 | tf_op jit(solution)/shard_map/while/body/eval_jaxpr/ppermute | solution.py:15
  103.6 6.2 collective-permute-start.1
  105.6 28.5 %slice-start = ((s8[8388608]{0:T(1024)(128)(4,1)}), s8[4194304]{0:T(1024)(128)(4,1)S(1)}, s32[]{:S(2)}) async-start(s8[8388608]{0:T(1024)(128)(4,1)} %bitcast.49), calls=%async_computation.1 | async-start | bytes 8388608 | tf_op jit(solution)/shard_map/while
  109.8 31.5 %slice-start.2 = ((s8[8388608]{0:T(1024)(128)(4,1)}), s8[4194304]{0:T(1024)(128)(4,1)S(1)}, s32[]{:S(2)}) async-start(s8[8388608]{0:T(1024)(128)(4,1)} %bitcast.51), calls=%async_computation.3 | async-start | bytes 8388608 | tf_op jit(solution)/shard_map/while
  158.3 26.0 %collective-permute-start = (f32[1,2,16,1,128,128]{5,4,3,2,1,0:T(8,128)}, f32[1,2,16,1,128,128]{5,4,3,2,1,0:T(8,128)}, u32[]{:S(2)}, u32[]{:S(2)}) collective-permute-start(f32[1,2,16,1,128,128]{5,4,3,2,1,0:T(8,128)} %get-tuple-element.260), channel_id=1, source_target_pairs={{0,1},{1,2},{2,3},{3,4},{4,5},{5,6},{6,7},{8,9},{9,10},{10,11},{11... | collective-permute-start | bytes 6291464 | tf_op jit(solution)/shard_map/while/body/eval_jaxpr/ppermute | solution.py:15
  181.5 6.2 collective-permute-start.1
  187.7 31.5 %slice-start.2 = ((s8[8388608]{0:T(1024)(128)(4,1)}), s8[4194304]{0:T(1024)(128)(4,1)S(1)}, s32[]{:S(2)}) async-start(s8[8388608]{0:T(1024)(128)(4,1)} %bitcast.51), calls=%async_computation.3 | async-start | bytes 8388608 | tf_op jit(solution)/shard_map/while
  236.3 26.0 %collective-permute-start = (f32[1,2,16,1,128,128]{5,4,3,2,1,0:T(8,128)}, f32[1,2,16,1,128,128]{5,4,3,2,1,0:T(8,128)}, u32[]{:S(2)}, u32[]{:S(2)}) collective-permute-start(f32[1,2,16,1,128,128]{5,4,3,2,1,0:T(8,128)} %get-tuple-element.260), channel_id=1, source_target_pairs={{0,1},{1,2},{2,3},{3,4},{4,5},{5,6},{6,7},{8,9},{9,10},{10,11},{11... | collective-permute-start | bytes 6291464 | tf_op jit(solution)/shard_map/while/body/eval_jaxpr/ppermute | solution.py:15
  259.5 6.2 collective-permute-start.1
  265.7 31.5 %slice-start.2 = ((s8[8388608]{0:T(1024)(128)(4,1)}), s8[4194304]{0:T(1024)(128)(4,1)S(1)}, s32[]{:S(2)}) async-start(s8[8388608]{0:T(1024)(128)(4,1)} %bitcast.51), calls=%async_computation.3 | async-start | bytes 8388608 | tf_op jit(solution)/shard_map/while
  314.2 26.0 %collective-permute-start = (f32[1,2,16,1,128,128]{5,4,3,2,1,0:T(8,128)}, f32[1,2,16,1,128,128]{5,4,3,2,1,0:T(8,128)}, u32[]{:S(2)}, u32[]{:S(2)}) collective-permute-start(f32[1,2,16,1,128,128]{5,4,3,2,1,0:T(8,128)} %get-tuple-element.260), channel_id=1, source_target_pairs={{0,1},{1,2},{2,3},{3,4},{4,5},{5,6},{6,7},{8,9},{9,10},{10,11},{11... | collective-permute-start | bytes 6291464 | tf_op jit(solution)/shard_map/while/body/eval_jaxpr/ppermute | solution.py:15
  337.4 6.2 collective-permute-start.1
  343.6 31.5 %slice-start.2 = ((s8[8388608]{0:T(1024)(128)(4,1)}), s8[4194304]{0:T(1024)(128)(4,1)S(1)}, s32[]{:S(2)}) async-start(s8[8388608]{0:T(1024)(128)(4,1)} %bitcast.51), calls=%async_computation.3 | async-start | bytes 8388608 | tf_op jit(solution)/shard_map/while
  392.2 26.0 %collective-permute-start = (f32[1,2,16,1,128,128]{5,4,3,2,1,0:T(8,128)}, f32[1,2,16,1,128,128]{5,4,3,2,1,0:T(8,128)}, u32[]{:S(2)}, u32[]{:S(2)}) collective-permute-start(f32[1,2,16,1,128,128]{5,4,3,2,1,0:T(8,128)} %get-tuple-element.260), channel_id=1, source_target_pairs={{0,1},{1,2},{2,3},{3,4},{4,5},{5,6},{6,7},{8,9},{9,10},{10,11},{11... | collective-permute-start | bytes 6291464 | tf_op jit(solution)/shard_map/while/body/eval_jaxpr/ppermute | solution.py:15
  415.4 6.2 collective-permute-start.1
  417.4 28.5 %slice-start = ((s8[8388608]{0:T(1024)(128)(4,1)}), s8[4194304]{0:T(1024)(128)(4,1)S(1)}, s32[]{:S(2)}) async-start(s8[8388608]{0:T(1024)(128)(4,1)} %bitcast.49), calls=%async_computation.1 | async-start | bytes 8388608 | tf_op jit(solution)/shard_map/while
  421.6 31.5 %slice-start.2 = ((s8[8388608]{0:T(1024)(128)(4,1)}), s8[4194304]{0:T(1024)(128)(4,1)S(1)}, s32[]{:S(2)}) async-start(s8[8388608]{0:T(1024)(128)(4,1)} %bitcast.51), calls=%async_computation.3 | async-start | bytes 8388608 | tf_op jit(solution)/shard_map/while
  468.5 31.3 %copy-start.4 = (f32[4]{0:T(128)S(1)}, f32[4]{0:T(128)}, u32[]{:S(2)}) copy-start(f32[4]{0:T(128)} %param.13) | copy-start | bytes 52
  (33 other events, 456.3 us)
Sparse Core Ops, SparseCore 0:
  563.5 155.4 all-gather.2
